TPU v7x, 32 devices: a whole 2x2x4 slice. The times are simulated.
32 devices in a mesh: task: 4 (over y, core), col: 8 (over z, x).
Axes of the slice: x: 2, y: 2, z: 4, core: 2. Of those that a mesh axis runs over, the one named last changes fastest.
Arguments:
- layer_inputs: bfloat16 [4, 1024, 8192], P('task', None, 'col'), may hold values from -6 to 6
- queries: bfloat16 [4, 1024, 8192], P('task', None, 'col'), may hold values from -1000 to 1000, as said below
- key_values: bfloat16 [4, 1024, 2048], P('task', 'col'), may hold values from -8 to 8, as said below
- out_grads: bfloat16 [4, 1024, 8192], P('task', None, 'col'), may hold values from -0.29882812 to 0.29882812
- lengths: int32 [4, 4], P('task'), may hold values from 1 to 512, 1024 in all within a row
- task_weights: bfloat16 [4, 8192, 2048], P('task', 'col'), may hold values from -6 to 6
Outputs:
- fisher: float32 [4, 8192, 2048], P('task', 'col')
- merged: bfloat16 [8192, 2048], P('col')
Inputs may be any that keep to these rules, and one draw needn't show every extreme that they name: `queries`: queries of every head for the tokens of each task. `key_values`: keys and values of every head for the tokens of each task.
All inputs are finite; a program needn't handle non-finite values.
Results may differ from a plain program's by a relative error of at most 0.02.
Values may be sent and summed in bfloat16 or wider, within the bound.
No kernel may reach another device: no remote copies, remote signals or barrier semaphores. Data moves between devices by JAX's collectives and lax.ppermute only.
A program may use at most 128 MiB of HBM per device.

v0:
```python
import jax
import jax.numpy as jnp
from jax import lax
from jax.sharding import PartitionSpec as P

KVH = 8
HD = 128
EPS = 1e-06
NEGATIVE = -1e30


def layout(lengths, count):
    ending = jnp.cumsum(lengths)
    starts = ending - lengths
    places = jnp.arange(count, dtype=jnp.int32)
    owner = jnp.sum((places[:, None] >= ending[None, :]).astype(jnp.int32), axis=1)
    allowed = (owner[:, None] == owner[None, :]) & (places[:, None] >= places[None, :])
    return (owner, starts, allowed)


def head_grads(head_query, head_keys, head_values, head_cotangent, allowed):
    factor = HD ** (-0.5)
    scores = jnp.dot(head_query, head_keys.T, preferred_element_type=jnp.float32) * factor
    scores = jnp.where(allowed, scores, NEGATIVE)
    highest = jnp.max(scores, axis=1, keepdims=True)
    summed = jnp.sum(jnp.exp(scores - highest), axis=1, keepdims=True)
    chances = jnp.where(
        allowed, jnp.exp(scores - highest - jnp.log(summed)), jnp.zeros_like(scores)
    )
    slopes = jnp.dot(head_cotangent, head_values.T, preferred_element_type=jnp.float32)
    offsets = jnp.sum(chances * slopes, axis=1, keepdims=True)
    score_grads = (chances * (slopes - offsets)).astype(jnp.bfloat16)
    value_grads = jnp.dot(
        chances.astype(jnp.bfloat16).T, head_cotangent, preferred_element_type=jnp.float32
    )
    key_grads = jnp.dot(score_grads.T, head_query, preferred_element_type=jnp.float32) * factor
    return jnp.concatenate([key_grads, value_grads], axis=1)


def seq_fisher(inputs, grads_all, owner, starts, number_seqs):
    window = inputs.shape[0] // 2
    last_start = inputs.shape[0] - window

    def one_seq(running, number):
        opening = jnp.clip(starts[number], 0, last_start)
        rows_in = lax.dynamic_slice_in_dim(inputs, opening, window, 0)
        rows_grad = lax.dynamic_slice_in_dim(grads_all, opening, window, 0)
        inside = lax.dynamic_slice_in_dim(owner, opening, window, 0) == number
        rows_grad = jnp.where(inside[:, None], rows_grad, jnp.zeros_like(rows_grad))
        gradient = jnp.dot(rows_in.T, rows_grad, preferred_element_type=jnp.float32)
        return (running + gradient * gradient, None)

    start_value = jnp.zeros((inputs.shape[1], grads_all.shape[1]), jnp.float32)
    running, unused = lax.scan(one_seq, start_value, jnp.arange(number_seqs, dtype=jnp.int32))
    return running


def body(layer_inputs, queries, key_values, out_grads, lengths, task_weights):
    devices = lax.axis_size("col")
    groups = devices // KVH
    pair_width = 2 * HD
    kv_width = key_values.shape[2]
    inputs = layer_inputs[0]
    count = inputs.shape[0]
    local_rows = key_values[0]
    copies = jnp.repeat(local_rows.reshape(local_rows.shape[0], KVH, pair_width), groups, axis=1)
    head_block = lax.all_to_all(copies, "col", split_axis=1, concat_axis=0, tiled=True).reshape(
        count, pair_width
    )
    owner, starts, allowed = layout(lengths[0], count)
    head_keys = head_block[:, :HD]
    head_values = head_block[:, HD:]
    local_queries = queries[0]
    local_cotangents = out_grads[0]
    partial_sum = jnp.zeros((count, pair_width), jnp.float32)
    for member in range(local_queries.shape[1] // HD):
        head_query = local_queries[:, member * HD : (member + 1) * HD]
        head_cotangent = local_cotangents[:, member * HD : (member + 1) * HD]
        partial_sum = partial_sum + head_grads(
            head_query, head_keys, head_values, head_cotangent, allowed
        )
    partial_value = partial_sum.astype(jnp.bfloat16)
    piece = lax.all_gather(partial_value, "col", axis=1, tiled=True)
    shards = piece.shape[1] // pair_width
    owners = jnp.arange(shards, dtype=jnp.int32) // groups
    selector = (owners[:, None] == jnp.arange(KVH, dtype=jnp.int32)[None, :]).astype(jnp.bfloat16)
    placed = jnp.einsum(
        "tnc,nh->thc",
        piece.reshape(count, shards, pair_width),
        selector,
        preferred_element_type=jnp.float32,
    )
    grads_all = placed.reshape(count, kv_width).astype(jnp.bfloat16)
    fisher = seq_fisher(inputs, grads_all, owner, starts, lengths.shape[1])
    weighted = fisher * task_weights[0].astype(jnp.float32)
    weighted_sum, fisher_sum = (
        lax.psum(weighted.astype(jnp.bfloat16), "task").astype(jnp.float32),
        lax.psum(fisher.astype(jnp.bfloat16), "task").astype(jnp.float32),
    )
    merged = (weighted_sum / (fisher_sum + EPS)).astype(jnp.bfloat16)
    return (fisher[None], merged)


def solution(mesh):
    in_specs = (
        P("task", None, "col"),
        P("task", None, "col"),
        P("task", "col", None),
        P("task", None, "col"),
        P("task", None),
        P("task", "col", None),
    )
    out_specs = (P("task", "col", None), P("col", None))
    return jax.shard_map(body, mesh=mesh, in_specs=in_specs, out_specs=out_specs, check_vma=False)
```

profile of v0, /device:TPU:0, one launch (start us, length us, event | category | flops | bytes accessed | tf_op | source)
XLA Modules:
  0.0 478.3 jit_solution(18037446713357013395)
XLA Ops:
  9.4 7.3 %all-to-all-start = ((bf16[128,8,256]{0,2,1:T(8,128)(2,1)}), bf16[128,8,256]{0,2,1:T(8,128)(2,1)S(1)}, u32[]{:S(2)}, u32[]{:S(2)}) async-start(bf16[128,8,256]{0,2,1:T(8,128)(2,1)} %bitcast.6), calls=%async_computation | async-start | bytes 1048576 | tf_op jit(solution)/shard_map/all_to_all | solution.py:67
  17.6 13.5 %all-to-all-done = bf16[128,8,256]{0,2,1:T(8,128)(2,1)S(1)} async-done(((bf16[128,8,256]{0,2,1:T(8,128)(2,1)}), bf16[128,8,256]{0,2,1:T(8,128)(2,1)S(1)}, u32[]{:S(2)}, u32[]{:S(2)}) %all-to-all-start) | async-done | bytes 524320 | tf_op jit(solution)/shard_map/all_to_all | solution.py:67
  31.4 3.6 fusion.104
  34.9 2.7 fusion.98
  37.6 2.6 fusion.92
  40.3 2.8 fusion.86
  43.8 2.7 fusion.74
  47.2 2.7 fusion.101
  49.9 2.7 fusion.95
  52.5 2.6 fusion.89
  55.2 2.7 fusion.107
  59.2 3.0 exponential_reduce_fusion
  64.5 15.9 %multiply_reduce_fusion = (f32[1024]{0:T(1024)S(1)}, f32[1024]{0:T(1024)S(1)}, f32[1024]{0:T(1024)S(1)}, f32[1024]{0:T(1024)S(1)}, f32[1024]{0:T(1024)S(1)}, /*i...) fusion(f32[1024]{0:T(1024)S(1)} %log.71, f32[1024]{0:T(1024)S(1)} %get-tuple-element.74, ...), kind=kOutput, calls=%fused_computation.13 | convolution fusion | flops 305127424 | bytes 42524672 | tf_op jit(solution)/shard_map/dot_general | solution.py:30
  82.1 2.2 fusion.31
  85.6 8.4 %exponential_reduce_fusion.1 = (f32[1024]{0:T(1024)S(1)}, f32[1024]{0:T(1024)S(1)}, f32[1024]{0:T(1024)S(1)}, f32[1024]{0:T(1024)S(1)}, f32[1024]{0:T(1024)S(1)}, /*index=5*/f32[1024,1024]{0,1:T(8,128)}) fusion(f32[1024,1024]{0,1:T(8,128)S(1)} %copy-done.4, f32[1024]{0:T(1024)S(1)} %get-tuple-element.71, s32[1024]{0:T(1024)S(1)} %convert_reduce_fusion, ...), kind=kOutput, calls=%fused_computation.20 | convolution fusion | flops 295693312 | bytes 25743360 | tf_op jit(solution)/shard_map/dot_general | solution.py:30
  96.1 4.2 fusion.40
  100.3 3.9 fusion.43
  104.2 4.1 fusion.28
  108.3 15.3 %multiply_reduce_fusion.1 = (f32[1024]{0:T(1024)S(1)}, f32[1024]{0:T(1024)S(1)}, f32[1024]{0:T(1024)S(1)}, f32[1024]{0:T(1024)S(1)}, f32[1024]{0:T(1024)S(1)}, /*index=5*/f32[1024,1024]{0,1:T(8,128)}) fusion(f32[1024]{0:T(1024)S(1)} %log.70, f32[1024]{0:T(1024)S(1)} %get-tuple-element.71, f32[1024,1024]{0,1:T(8,128)} %fusion.74, ...), kind=kOutput, calls=%fused_computation.18 | convolution fusion | flops 305130496 | bytes 38338560 | tf_op jit(solution)/shard_map/dot_general | solution.py:30
  125.7 4.9 %multiply_reduce_fusion.3 = (f32[1024]{0:T(1024)S(1)}, f32[1024,1024]{0,1:T(8,128)}) fusion(f32[1024]{0:T(1024)S(1)} %log.68, f32[1024]{0:T(1024)S(1)} %get-tuple-element.69, f32[1024,1024]{0,1:T(8,128)S(1)} %copy-done.3, s32[1024]{0:T(1024)S(1)} %convert_reduce_fusion, bf16[1024,256]{1,0:T(8,128)(2,1)S(1)} %bitcast.48, bf16[1024,1024]{1,0:T(8,128)(2,1)} %bitcast.78), kind=kOutput, calls=%fused_computation.28 | convolution fusion | flops 278920192 | bytes 8933376 | tf_op jit(solution)/shard_map/dot_general | solution.py:30
  155.9 71.9 %all-gather.2.cloned.1.call-done = bf16[1024,2048]{0,1:T(8,128)(2,1)} async-done(((bf16[1024,256]{0,1:T(8,128)(2,1)}), bf16[1024,2048]{0,1:T(8,128)(2,1)}) %all-gather.2.cloned.1.call-update) | async-done | bytes 4194320 | tf_op jit(solution)/shard_map/all_gather | solution.py:83
  227.8 6.9 %copy.15 = bf16[1024,8,256]{2,1,0:T(8,128)(2,1)} copy(bf16[1024,8,256]{0,2,1:T(8,128)(2,1)} %bitcast.51) | data formatting | bytes 8388608 | tf_op jit(solution)/shard_map/reshape | solution.py:89
  234.7 3.4 convolution_convert_fusion
  238.1 3.5 copy.16
  241.6 57.4 %while.11 = (s32[]{:T(128)}, f32[1024,2048]{1,0:T(8,128)}, s32[4]{0:T(128)S(1)}, s32[4]{0:T(128)S(1)}, bf16[1024,1024]{1,0:T(8,128)(2,1)S(1)}, /*index=5*/s32[10...) while((s32[]{:T(128)}, f32[1024,2048]{1,0:T(8,128)}, ...), condition=%wide.region_27.28_spmd.clone, body=%wide.region_26.27_spmd.clone.sunk | while | flops 2154824192 | bytes 19927264 | solution.py:54
  246.2 7.9 %select_add_fusion.2 = f32[1024,2048]{1,0:T(8,128)} fusion(f32[1024,2048]{1,0:T(8,128)} %get-tuple-element.166, pred[]{:T(512)S(6)} %compare.5, bf16[1024,2048]{1,0:T(8,128)(2,1)} %get-tuple-element.183, s32[]{:T(128)} %bitcast.30, pred[512]{0:T(512)(128)(4,1)S(1)} %dynamic-slice_compare_fusion.2, bf16[1024,1024]{1,0:T(8,128)(2,1)S(1)} %get-tuple-element.181), kind=kOutput, calls=%fused_computation.clone.1 | convolution fusion | flops 2154823680 | bytes 19924480 | tf_op jit(solution)/shard_map/while/body/eval_jaxpr/dot_general | solution.py:50
  258.8 10.3 %select_add_fusion.2 = f32[1024,2048]{1,0:T(8,128)} fusion(f32[1024,2048]{1,0:T(8,128)} %get-tuple-element.166, pred[]{:T(512)S(6)} %compare.5, bf16[1024,2048]{1,0:T(8,128)(2,1)} %get-tuple-element.183, s32[]{:T(128)} %bitcast.30, pred[512]{0:T(512)(128)(4,1)S(1)} %dynamic-slice_compare_fusion.2, bf16[1024,1024]{1,0:T(8,128)(2,1)S(1)} %get-tuple-element.181), kind=kOutput, calls=%fused_computation.clone.1 | convolution fusion | flops 2154823680 | bytes 19924480 | tf_op jit(solution)/shard_map/while/body/eval_jaxpr/dot_general | solution.py:50
  273.8 10.3 %select_add_fusion.2 = f32[1024,2048]{1,0:T(8,128)} fusion(f32[1024,2048]{1,0:T(8,128)} %get-tuple-element.166, pred[]{:T(512)S(6)} %compare.5, bf16[1024,2048]{1,0:T(8,128)(2,1)} %get-tuple-element.183, s32[]{:T(128)} %bitcast.30, pred[512]{0:T(512)(128)(4,1)S(1)} %dynamic-slice_compare_fusion.2, bf16[1024,1024]{1,0:T(8,128)(2,1)S(1)} %get-tuple-element.181), kind=kOutput, calls=%fused_computation.clone.1 | convolution fusion | flops 2154823680 | bytes 19924480 | tf_op jit(solution)/shard_map/while/body/eval_jaxpr/dot_general | solution.py:50
  288.7 10.3 %select_add_fusion.2 = f32[1024,2048]{1,0:T(8,128)} fusion(f32[1024,2048]{1,0:T(8,128)} %get-tuple-element.166, pred[]{:T(512)S(6)} %compare.5, bf16[1024,2048]{1,0:T(8,128)(2,1)} %get-tuple-element.183, s32[]{:T(128)} %bitcast.30, pred[512]{0:T(512)(128)(4,1)S(1)} %dynamic-slice_compare_fusion.2, bf16[1024,1024]{1,0:T(8,128)(2,1)S(1)} %get-tuple-element.181), kind=kOutput, calls=%fused_computation.clone.1 | convolution fusion | flops 2154823680 | bytes 19924480 | tf_op jit(solution)/shard_map/while/body/eval_jaxpr/dot_general | solution.py:50
  299.0 12.8 %fusion.7 = (bf16[1024,2048]{1,0:T(8,128)(2,1)}, bf16[1024,2048]{1,0:T(8,128)(2,1)}) fusion(f32[1024,2048]{1,0:T(8,128)} %get-tuple-element.39, bf16[1,1024,2048]{2,1,0:T(8,128)(2,1)} %param.13), kind=kLoop, calls=%fused_computation.10 | loop fusion | flops 8388608 | bytes 20971520 | tf_op jit(solution)/shard_map/convert_element_type | solution.py:97
  311.8 151.6 %all-reduce.3.cloned.1.call-done = (bf16[1024,2048]{1,0:T(8,128)(2,1)}, bf16[1024,2048]{1,0:T(8,128)(2,1)}) async-done(((bf16[1024,2048]{1,0:T(8,128)(2,1)}, bf16[1024,2048]{1,0:T(8,128)(2,1)}), (bf16[1024,2048]{1,0:T(8,128)(2,1)}, bf16[1024,2048]{1,0:T(8,128)(2,1)})) %all-reduce.3.cloned.1.call-update) | async-done | bytes 8388624 | tf_op jit(solution)/shard_map/psum | solution.py:98
  463.4 7.9 %divide_convert_fusion = bf16[1024,2048]{1,0:T(8,128)(2,1)} fusion(bf16[1024,2048]{1,0:T(8,128)(2,1)} %get-tuple-element.100, bf16[1024,2048]{1,0:T(8,128)(2,1)} %get-tuple-element.101), kind=kLoop, calls=%fused_computation.11 | loop fusion | flops 10485760 | bytes 12582912 | tf_op jit(solution)/shard_map/convert_element_type | solution.py:100
  (100 shorter events, 48.7 us)
Async XLA Ops:
  7.2 27.8 %copy-start.16 = (bf16[1,1024,1024]{2,1,0:T(8,128)(2,1)S(1)}, bf16[1,1024,1024]{2,1,0:T(8,128)(2,1)}, u32[]{:S(2)}) copy-start(bf16[1,1024,1024]{2,1,0:T(8,128)(2,1)} %param.9) | copy-start | bytes 6291460
  9.4 21.8 %all-to-all-start = ((bf16[128,8,256]{0,2,1:T(8,128)(2,1)}), bf16[128,8,256]{0,2,1:T(8,128)(2,1)S(1)}, u32[]{:S(2)}, u32[]{:S(2)}) async-start(bf16[128,8,256]{0,2,1:T(8,128)(2,1)} %bitcast.6), calls=%async_computation | async-start | bytes 1048576 | tf_op jit(solution)/shard_map/all_to_all | solution.py:67
  16.6 211.2 %all-gather.2.cloned.1.call-start = ((), (), s32[]{:S(2)}) async-start(), calls=%async_computation.1 | async-start | bytes 4718592 | tf_op jit(solution)/shard_map/all_gather | solution.py:83
  43.8 3.4 copy-start.17
  59.2 4.1 copy-start.1
  80.3 4.0 copy-start.9
  82.0 2.4 copy-start.4
  82.0 3.6 copy-start.6
  85.6 8.4 %copy-start.12 = (f32[1024,1024]{0,1:T(8,128)S(1)}, f32[1024,1024]{0,1:T(8,128)}, u32[]{:S(2)}) copy-start(f32[1024,1024]{0,1:T(8,128)} %fusion.92) | copy-start | bytes 12582916
  104.2 4.1 copy-start.3
  125.7 4.9 %copy-start.15 = (f32[1024,1024]{0,1:T(8,128)S(1)}, f32[1024,1024]{0,1:T(8,128)}, u32[]{:S(2)}) copy-start(f32[1024,1024]{0,1:T(8,128)} %fusion.107) | copy-start | bytes 12582916
  130.6 2.2 copy-start.13
  130.7 3.5 copy-start.14
  134.1 2.2 copy-start.10
  134.1 3.5 copy-start.11
  137.6 2.2 copy-start.7
  137.6 3.5 copy-start.8
  141.0 2.2 copy-start.2
  141.0 3.5 copy-start.23
  144.5 2.2 copy-start.24
  146.7 2.2 copy-start.5
  146.7 3.5 copy-start.25
  150.2 2.2 copy-start.22
  152.4 1.7 copy-start.18
  152.4 1.7 copy-start.19
  152.4 1.7 copy-start.20
  154.1 1.7 copy-start.21
  155.8 307.6 %all-reduce.3.cloned.1.call-start = ((), (), s32[]{:S(2)}) async-start(), calls=%async_computation.2 | async-start | bytes 16777216 | tf_op jit(solution)/shard_map/psum | solution.py:98
  238.1 3.5 copy-start
Sparse Core Ops, SparseCore 0:
  155.9 71.8 all-gather.1
  312.0 151.3 all-reduce.2
where the time goes:
time: 486 us; the launch traced here: 478 us
  waiting for transfers between devices  237 us (49%)
  matrix products  148 us (30%)
  other arithmetic  31 us (6%)
  local copies, waits for them, and re-layouts  30.2 us (6%)
  between operations  14.6 us (3%)
  loops' own time  10.6 us (2%)
  starting transfers between devices  7.36 us (2%)
    psum x1, waiting for transfers between devices, body(): lax.psum(fisher.astype(jnp.bfloat16), 'task').astype(jnp.float32)  152 us
    all_gather x1, waiting for transfers between devices, body(): piece = lax.all_gather(partial_value, 'col', axis=1, tiled=True)  71.9 us
    dot_general x8, matrix products, head_grads(): jnp.dot(head_cotangent, head_values.T, preferred_element_type=jnp.float32)  55.1 us
    dot_general x4, matrix products, one_seq(): gradient = jnp.dot(rows_in.T, rows_grad, preferred_element_type=jnp.float32)  38.8 us
    dot_general x8, matrix products, head_grads(): jnp.dot(chances.astype(jnp.bfloat16).T, head_cotangent, preferred_element...  20.8 us
    unnamed x54, local copies, waits for them, and re-layouts  18.1 us
    dot_general x8, matrix products, head_grads(): jnp.dot(head_query, head_keys.T, preferred_element_type=jnp.float32)  17.1 us
    all_to_all x1, waiting for transfers between devices, body(): lax.all_to_all(copies, 'col', split_axis=1, concat_axis=0, tiled=True)  13.5 us
  transfers between devices with their start and end apart: 3, of which 3 were waited for; matrix products, arithmetic and copies ran while one was open for 0% of the time, Pallas kernels for 0%

commit v1 on v0

--- a/solution.py
+++ b/solution.py
@@ -7,6 +7,12 @@
 HD = 128
 EPS = 1e-06
 NEGATIVE = -1e30
+
+
+def summed_here(x, axis):
+    parts = lax.all_gather(x, axis, axis=0, tiled=False)
+    total = parts.sum(axis=0)
+    return total
 
 
 def layout(lengths, count):
@@ -95,7 +101,7 @@
     weighted = fisher * task_weights[0].astype(jnp.float32)
     weighted_sum, fisher_sum = (
         lax.psum(weighted.astype(jnp.bfloat16), "task").astype(jnp.float32),
-        lax.psum(fisher.astype(jnp.bfloat16), "task").astype(jnp.float32),
+        summed_here(fisher.astype(jnp.bfloat16), "task").astype(jnp.float32),
     )
     merged = (weighted_sum / (fisher_sum + EPS)).astype(jnp.bfloat16)
     return (fisher[None], merged)

time: 486 us -> 527 us (1.084)
  waiting for transfers between devices: 237 us -> 266 us
  other arithmetic: 31 us -> 43.8 us
    all_gather x0 -> x1, waiting for transfers between devices: none -> 104 us  [summed_here(): parts = lax.all_gather(x, axis, axis=0, tiled=False)]
    psum x1, waiting for transfers between devices: 152 us -> 75.7 us  [body(): lax.psum(weighted.astype(jnp.bfloat16), 'task').astype(jnp.float32)]
    reduce_sum x0 -> x1, other arithmetic: none -> 12.8 us  [summed_here(): total = parts.sum(axis=0)]
  transfers between devices with their start and end apart: 3 -> 4, of which waited for: 3 -> 4; matrix products, arithmetic and copies ran while one was open for 0% -> 3% of each run, Pallas kernels for 0% -> 0%
where the time goes in v1:
time: 527 us; the launch traced here: 520 us
  waiting for transfers between devices  266 us (50%)
  matrix products  148 us (28%)
  other arithmetic  43.8 us (8%)
  local copies, waits for them, and re-layouts  30.2 us (6%)
  between operations  14.3 us (3%)
  loops' own time  10.6 us (2%)
  starting transfers between devices  7.4 us (1%)
    all_gather x1, waiting for transfers between devices, summed_here(): parts = lax.all_gather(x, axis, axis=0, tiled=False)  104 us
    psum x1, waiting for transfers between devices, body(): lax.psum(weighted.astype(jnp.bfloat16), 'task').astype(jnp.float32)  75.7 us
    all_gather x1, waiting for transfers between devices, body(): piece = lax.all_gather(partial_value, 'col', axis=1, tiled=True)  71.9 us
    dot_general x8, matrix products, head_grads(): jnp.dot(head_cotangent, head_values.T, preferred_element_type=jnp.float32)  55.1 us
    dot_general x4, matrix products, one_seq(): gradient = jnp.dot(rows_in.T, rows_grad, preferred_element_type=jnp.float32)  38.8 us
    dot_general x8, matrix products, head_grads(): jnp.dot(chances.astype(jnp.bfloat16).T, head_cotangent, preferred_element...  20.8 us
    unnamed x54, local copies, waits for them, and re-layouts  18.1 us
    dot_general x8, matrix products, head_grads(): jnp.dot(head_query, head_keys.T, preferred_element_type=jnp.float32)  17.1 us
  transfers between devices with their start and end apart: 4, of which 4 were waited for; matrix products, arithmetic and copies ran while one was open for 3% of the time, Pallas kernels for 0%

profile of v1, /device:TPU:0, one launch (start us, length us, event | category | flops | bytes accessed | tf_op | source)
XLA Modules:
  0.0 519.6 jit_solution(5383115996678895686)
XLA Ops:
  9.4 7.3 %all-to-all-start = ((bf16[128,8,256]{0,2,1:T(8,128)(2,1)}), bf16[128,8,256]{0,2,1:T(8,128)(2,1)S(1)}, u32[]{:S(2)}, u32[]{:S(2)}) async-start(bf16[128,8,256]{0,2,1:T(8,128)(2,1)} %bitcast.6), calls=%async_computation | async-start | bytes 1048576 | tf_op jit(solution)/shard_map/all_to_all | solution.py:73
  17.6 13.5 %all-to-all-done = bf16[128,8,256]{0,2,1:T(8,128)(2,1)S(1)} async-done(((bf16[128,8,256]{0,2,1:T(8,128)(2,1)}), bf16[128,8,256]{0,2,1:T(8,128)(2,1)S(1)}, u32[]{:S(2)}, u32[]{:S(2)}) %all-to-all-start) | async-done | bytes 524320 | tf_op jit(solution)/shard_map/all_to_all | solution.py:73
  31.4 3.6 fusion.104
  34.9 2.7 fusion.98
  37.6 2.6 fusion.92
  40.3 2.8 fusion.86
  43.8 2.7 fusion.74
  47.2 2.7 fusion.101
  49.9 2.7 fusion.95
  55.2 2.7 fusion.107
  59.2 3.0 exponential_reduce_fusion
  64.5 15.9 %multiply_reduce_fusion = (f32[1024]{0:T(1024)S(1)}, f32[1024]{0:T(1024)S(1)}, f32[1024]{0:T(1024)S(1)}, f32[1024]{0:T(1024)S(1)}, f32[1024]{0:T(1024)S(1)}, /*i...) fusion(f32[1024]{0:T(1024)S(1)} %log.71, f32[1024]{0:T(1024)S(1)} %get-tuple-element.74, ...), kind=kOutput, calls=%fused_computation.13 | convolution fusion | flops 305127424 | bytes 42524672 | tf_op jit(solution)/shard_map/dot_general | solution.py:36
  85.6 8.4 %exponential_reduce_fusion.1 = (f32[1024]{0:T(1024)S(1)}, f32[1024]{0:T(1024)S(1)}, f32[1024]{0:T(1024)S(1)}, f32[1024]{0:T(1024)S(1)}, f32[1024]{0:T(1024)S(1)}, /*index=5*/f32[1024,1024]{0,1:T(8,128)}) fusion(f32[1024,1024]{0,1:T(8,128)S(1)} %copy-done.4, f32[1024]{0:T(1024)S(1)} %get-tuple-element.71, s32[1024]{0:T(1024)S(1)} %convert_reduce_fusion, ...), kind=kOutput, calls=%fused_computation.20 | convolution fusion | flops 295693312 | bytes 25743360 | tf_op jit(solution)/shard_map/dot_general | solution.py:36
  96.1 4.2 fusion.40
  100.3 3.9 fusion.43
  104.2 4.1 fusion.28
  108.3 15.3 %multiply_reduce_fusion.1 = (f32[1024]{0:T(1024)S(1)}, f32[1024]{0:T(1024)S(1)}, f32[1024]{0:T(1024)S(1)}, f32[1024]{0:T(1024)S(1)}, f32[1024]{0:T(1024)S(1)}, /*index=5*/f32[1024,1024]{0,1:T(8,128)}) fusion(f32[1024]{0:T(1024)S(1)} %log.70, f32[1024]{0:T(1024)S(1)} %get-tuple-element.71, f32[1024,1024]{0,1:T(8,128)} %fusion.74, ...), kind=kOutput, calls=%fused_computation.18 | convolution fusion | flops 305130496 | bytes 38338560 | tf_op jit(solution)/shard_map/dot_general | solution.py:36
  125.7 4.9 multiply_reduce_fusion.3
  155.9 71.9 %all-gather.4.cloned.1.call-done = bf16[1024,2048]{0,1:T(8,128)(2,1)} async-done(((bf16[1024,256]{0,1:T(8,128)(2,1)}), bf16[1024,2048]{0,1:T(8,128)(2,1)}) %all-gather.4.cloned.1.call-update) | async-done | bytes 4194320 | tf_op jit(solution)/shard_map/all_gather | solution.py:89
  227.8 6.9 %copy.15 = bf16[1024,8,256]{2,1,0:T(8,128)(2,1)} copy(bf16[1024,8,256]{0,2,1:T(8,128)(2,1)} %bitcast.53) | data formatting | bytes 8388608 | tf_op jit(solution)/shard_map/reshape | solution.py:95
  234.7 3.4 convolution_convert_fusion
  238.1 3.5 copy.16
  241.6 57.4 %while.11 = (s32[]{:T(128)}, f32[1024,2048]{1,0:T(8,128)}, s32[4]{0:T(128)S(1)}, s32[4]{0:T(128)S(1)}, bf16[1024,1024]{1,0:T(8,128)(2,1)S(1)}, /*index=5*/s32[10...) while((s32[]{:T(128)}, f32[1024,2048]{1,0:T(8,128)}, ...), condition=%wide.region_27.28_spmd.clone, body=%wide.region_26.27_spmd.clone.sunk | while | flops 2154824192 | bytes 19927264 | solution.py:60
  246.2 7.9 %select_add_fusion.2 = f32[1024,2048]{1,0:T(8,128)} fusion(f32[1024,2048]{1,0:T(8,128)} %get-tuple-element.164, pred[]{:T(512)S(6)} %compare.5, bf16[1024,2048]{1,0:T(8,128)(2,1)} %get-tuple-element.181, s32[]{:T(128)} %bitcast.31, pred[512]{0:T(512)(128)(4,1)S(1)} %dynamic-slice_compare_fusion.2, bf16[1024,1024]{1,0:T(8,128)(2,1)S(1)} %get-tuple-element.179), kind=kOutput, calls=%fused_computation.clone.1 | convolution fusion | flops 2154823680 | bytes 19924480 | tf_op jit(solution)/shard_map/while/body/eval_jaxpr/dot_general | solution.py:56
  258.8 10.3 %select_add_fusion.2 = f32[1024,2048]{1,0:T(8,128)} fusion(f32[1024,2048]{1,0:T(8,128)} %get-tuple-element.164, pred[]{:T(512)S(6)} %compare.5, bf16[1024,2048]{1,0:T(8,128)(2,1)} %get-tuple-element.181, s32[]{:T(128)} %bitcast.31, pred[512]{0:T(512)(128)(4,1)S(1)} %dynamic-slice_compare_fusion.2, bf16[1024,1024]{1,0:T(8,128)(2,1)S(1)} %get-tuple-element.179), kind=kOutput, calls=%fused_computation.clone.1 | convolution fusion | flops 2154823680 | bytes 19924480 | tf_op jit(solution)/shard_map/while/body/eval_jaxpr/dot_general | solution.py:56
  273.8 10.3 %select_add_fusion.2 = f32[1024,2048]{1,0:T(8,128)} fusion(f32[1024,2048]{1,0:T(8,128)} %get-tuple-element.164, pred[]{:T(512)S(6)} %compare.5, bf16[1024,2048]{1,0:T(8,128)(2,1)} %get-tuple-element.181, s32[]{:T(128)} %bitcast.31, pred[512]{0:T(512)(128)(4,1)S(1)} %dynamic-slice_compare_fusion.2, bf16[1024,1024]{1,0:T(8,128)(2,1)S(1)} %get-tuple-element.179), kind=kOutput, calls=%fused_computation.clone.1 | convolution fusion | flops 2154823680 | bytes 19924480 | tf_op jit(solution)/shard_map/while/body/eval_jaxpr/dot_general | solution.py:56
  288.7 10.3 %select_add_fusion.2 = f32[1024,2048]{1,0:T(8,128)} fusion(f32[1024,2048]{1,0:T(8,128)} %get-tuple-element.164, pred[]{:T(512)S(6)} %compare.5, bf16[1024,2048]{1,0:T(8,128)(2,1)} %get-tuple-element.181, s32[]{:T(128)} %bitcast.31, pred[512]{0:T(512)(128)(4,1)S(1)} %dynamic-slice_compare_fusion.2, bf16[1024,1024]{1,0:T(8,128)(2,1)S(1)} %get-tuple-element.179), kind=kOutput, calls=%fused_computation.clone.1 | convolution fusion | flops 2154823680 | bytes 19924480 | tf_op jit(solution)/shard_map/while/body/eval_jaxpr/dot_general | solution.py:56
  299.0 12.8 %fusion.7 = (bf16[1024,2048]{1,0:T(8,128)(2,1)}, bf16[1024,2048]{1,0:T(8,128)(2,1)}) fusion(f32[1024,2048]{1,0:T(8,128)} %get-tuple-element.39, bf16[1,1024,2048]{2,1,0:T(8,128)(2,1)} %param.13), kind=kLoop, calls=%fused_computation.10 | loop fusion | flops 8388608 | bytes 20971520 | tf_op jit(solution)/shard_map/convert_element_type | solution.py:103
  312.6 103.8 %all-gather.6.cloned.1.call-done = bf16[4096,2048]{1,0:T(8,128)(2,1)} async-done(((bf16[1024,2048]{1,0:T(8,128)(2,1)}), bf16[4096,2048]{1,0:T(8,128)(2,1)}) %all-gather.6.cloned.1.call-update) | async-done | bytes 16777232 | tf_op jit(solution)/shard_map/all_gather | solution.py:13
  416.4 12.8 %reduce_sum.182 = bf16[1024,2048]{1,0:T(8,128)(2,1)} reduce(bf16[4,1024,2048]{2,1,0:T(8,128)(2,1)} %bitcast.50, bf16[]{:T(256)} %constant.46.clone.1), dimensions={0}, to_apply=%region_29.30 | reduce | flops 6291456 | bytes 20971522 | tf_op jit(solution)/shard_map/reduce_sum | solution.py:14
  429.2 75.7 %all-reduce.2.cloned.1.call-done = bf16[1024,2048]{1,0:T(8,128)(2,1)} async-done(((bf16[1024,2048]{1,0:T(8,128)(2,1)}), bf16[1024,2048]{1,0:T(8,128)(2,1)}) %all-reduce.2.cloned.1.call-update) | async-done | bytes 4194320 | tf_op jit(solution)/shard_map/psum | solution.py:103
  504.9 7.9 %divide_convert_fusion = bf16[1024,2048]{1,0:T(8,128)(2,1)} fusion(bf16[1024,2048]{1,0:T(8,128)(2,1)} %reduce_sum.182, bf16[1024,2048]{1,0:T(8,128)(2,1)} %all-reduce.2.cloned.1.call-done), kind=kLoop, calls=%fused_computation.11 | loop fusion | flops 10485760 | bytes 12582912 | tf_op jit(solution)/shard_map/convert_element_type | solution.py:106
  (104 shorter events, 54.3 us)
Async XLA Ops:
  7.2 27.8 %copy-start.16 = (bf16[1,1024,1024]{2,1,0:T(8,128)(2,1)S(1)}, bf16[1,1024,1024]{2,1,0:T(8,128)(2,1)}, u32[]{:S(2)}) copy-start(bf16[1,1024,1024]{2,1,0:T(8,128)(2,1)} %param.9) | copy-start | bytes 6291460
  9.4 21.8 %all-to-all-start = ((bf16[128,8,256]{0,2,1:T(8,128)(2,1)}), bf16[128,8,256]{0,2,1:T(8,128)(2,1)S(1)}, u32[]{:S(2)}, u32[]{:S(2)}) async-start(bf16[128,8,256]{0,2,1:T(8,128)(2,1)} %bitcast.6), calls=%async_computation | async-start | bytes 1048576 | tf_op jit(solution)/shard_map/all_to_all | solution.py:73
  16.6 211.2 %all-gather.4.cloned.1.call-start = ((), (), s32[]{:S(2)}) async-start(), calls=%async_computation.1 | async-start | bytes 4718592 | tf_op jit(solution)/shard_map/all_gather | solution.py:89
  43.7 3.4 copy-start.17
  59.2 4.1 copy-start.1
  80.3 4.0 copy-start.9
  82.0 2.4 copy-start.4
  82.0 3.6 copy-start.6
  85.6 8.4 %copy-start.12 = (f32[1024,1024]{0,1:T(8,128)S(1)}, f32[1024,1024]{0,1:T(8,128)}, u32[]{:S(2)}) copy-start(f32[1024,1024]{0,1:T(8,128)} %fusion.92) | copy-start | bytes 12582916
  104.2 4.1 copy-start.3
  125.7 4.9 copy-start.15
  130.6 2.2 copy-start.13
  130.7 3.5 copy-start.14
  134.1 2.2 copy-start.10
  134.1 3.5 copy-start.11
  137.6 2.2 copy-start.7
  137.6 3.5 copy-start.8
  141.0 2.2 copy-start.2
  141.0 3.5 copy-start.23
  144.5 2.2 copy-start.24
  146.7 2.2 copy-start.5
  146.7 3.5 copy-start.25
  150.2 2.2 copy-start.22
  152.4 1.7 copy-start.18
  152.4 1.7 copy-start.19
  152.4 1.7 copy-start.20
  154.1 1.7 copy-start.21
  155.8 260.6 %all-gather.6.cloned.1.call-start = ((), (), s32[]{:S(2)}) async-start(), calls=%async_computation.3 | async-start | bytes 20971520 | tf_op jit(solution)/shard_map/all_gather | solution.py:13
  238.1 3.5 copy-start
  311.8 193.1 %all-reduce.2.cloned.1.call-start = ((), (), s32[]{:S(2)}) async-start(), calls=%async_computation.2 | async-start | bytes 8388608 | tf_op jit(solution)/shard_map/psum | solution.py:103
Sparse Core Ops, SparseCore 0:
  155.9 71.8 all-gather.3
  311.9 104.4 all-gather.5
  419.4 85.4 all-reduce.1
